TPU v7x, 32 devices: a whole 2x2x4 slice. The times are simulated.
32 devices in a mesh: section: 4 (over x, core), shard: 2 (over y), replica: 4 (over z).
Axes of the slice: x: 2, y: 2, z: 4, core: 2. Of those that a mesh axis runs over, the one named last changes fastest.
Arguments:
- acts_fwd: bfloat16 [4, 1024, 4096], P('section', ('shard', 'replica')), may hold values from -30 to 30
- pos_fwd: int32 [4, 1024], P('section', ('shard', 'replica')), may hold values from 0 to 2047
- saved_acts: bfloat16 [4, 1024, 4096], P('section', ('shard', 'replica')), may hold values from -30 to 30
- pos_bwd: int32 [4, 1024], P('section', ('shard', 'replica')), may hold values from 0 to 2047
- grads_in: bfloat16 [4, 1024, 4096], P('section', ('shard', 'replica')), may hold values from -6 to 6
- key_cotan: bfloat16 [4, 1024, 512], P('section', ('shard', 'replica')), may hold values from -6 to 6
- weight: bfloat16 [4, 4096, 512], P('section', 'shard'), may hold values from -0.09375 to 0.09375
- gain: float32 [4, 4096], P('section'), may hold values from 0.1 to 1.9
Outputs:
- keys: bfloat16 [4, 1024, 512], P('section', ('shard', 'replica'))
- grad_out: bfloat16 [4, 1024, 4096], P('section', ('shard', 'replica'))
- weight_grad: float32 [4, 4096, 512], P('section', 'shard')
All inputs are finite; a program needn't handle non-finite values.
Results may differ from a plain program's by a relative error of at most 0.0058.
Values may be sent and summed in bfloat16 or wider, within the bound.
A program may use at most 64 MiB of HBM per device.

v0:
```python
import jax
import jax.numpy as jnp
from jax import lax
from jax.sharding import PartitionSpec as P

HEAD = 128


def from_behind(x, axis, by):
    size = lax.axis_size(axis)
    pairs = [(i, i + by) for i in range(size) if 0 <= i + by < size]
    return lax.ppermute(x, axis, pairs)


def rope_tables(positions):
    index = jnp.arange(HEAD // 2, dtype=jnp.float32)
    rate = 500000.0 ** (-(2.0 * index) / HEAD)
    angle = positions.astype(jnp.float32)[:, None] * rate[None, :]
    return (jnp.cos(angle), jnp.sin(angle))


def rotate(values, cosine, sine_part, orient):
    count = values.shape[0]
    heads = values.shape[1] // HEAD
    shaped = values.reshape(count, heads, HEAD)
    first_half = shaped[..., : HEAD // 2]
    second_half = shaped[..., HEAD // 2 :]
    cos_b = cosine[:, None, :]
    sin_b = orient * sine_part[:, None, :]
    joined = jnp.concatenate(
        [first_half * cos_b - second_half * sin_b, second_half * cos_b + first_half * sin_b], -1
    )
    return joined.reshape(count, heads * HEAD)


def normalize(stream, gain_row):
    values = stream.astype(jnp.float32)
    inverse = lax.rsqrt(jnp.mean(values * values, -1, keepdims=True) + 1e-05)
    return (values * inverse * gain_row[None, :], inverse, values)


def per_device(acts_fwd, pos_fwd, saved_acts, pos_bwd, grads_in, key_cotan, weight, gain):
    section_pos = lax.axis_index("section")
    section_count = lax.axis_size("section")
    came_fwd = from_behind(acts_fwd, "section", 1)
    stream = jnp.where(section_pos == 0, acts_fwd, came_fwd)[0]
    came_bwd = from_behind(grads_in, "section", -1)
    arrived = jnp.where(section_pos == section_count - 1, grads_in, came_bwd)[0]
    gain_row = gain[0]
    local_rows = weight[0]
    normed = normalize(stream, gain_row)[0].astype(jnp.bfloat16)
    back_f, inverse, saved_f = normalize(saved_acts[0], gain_row)
    back_normed = back_f.astype(jnp.bfloat16)
    cos_b, sin_b = rope_tables(pos_bwd[0])
    key_grad = rotate(key_cotan[0].astype(jnp.float32), cos_b, sin_b, -1.0).astype(jnp.bfloat16)
    tok_rows = normed.shape[0]
    gathered = lax.all_gather(local_rows, "shard", axis=0, tiled=True)
    projected = jnp.dot(normed, gathered, preferred_element_type=jnp.float32)
    normed_grad = lax.dot_general(
        key_grad, gathered, (((1,), (1,)), ((), ())), preferred_element_type=jnp.float32
    )
    cosine, sine_part = rope_tables(pos_fwd[0])
    keys = rotate(projected, cosine, sine_part, 1.0).astype(jnp.bfloat16)
    scaled = normed_grad * gain_row[None, :]
    stream_grad = inverse * scaled - saved_f * inverse**3 * jnp.mean(
        saved_f * scaled, -1, keepdims=True
    )
    grad_out = (arrived.astype(jnp.float32) + stream_grad).astype(jnp.bfloat16)
    shard_count = lax.axis_size("shard")
    replica_count = lax.axis_size("replica")
    owned_rows = local_rows.shape[0]
    slice_rows = (owned_rows + replica_count - 1) // replica_count
    padded_width = slice_rows * replica_count
    padded_norm = back_normed.reshape(tok_rows, shard_count, owned_rows)
    padded_norm = jnp.pad(padded_norm, ((0, 0), (0, 0), (0, padded_width - owned_rows)))
    padded_norm = padded_norm.reshape(tok_rows, shard_count * padded_width)
    term = lax.dot_general(
        padded_norm, key_grad, (((0,), (0,)), ((), ())), preferred_element_type=jnp.float32
    )
    rounded = lax.optimization_barrier(term.astype(jnp.bfloat16))
    slice_sum = lax.psum_scatter(
        rounded.astype(jnp.float32), ("shard", "replica"), scatter_dimension=0, tiled=True
    )
    collected = lax.all_gather(slice_sum, "replica", axis=0, tiled=True)
    summed = collected[:owned_rows]
    token_total = tok_rows * shard_count * replica_count
    weight_grad = summed * float(token_total) ** (-0.5)
    return (keys[None], grad_out[None], weight_grad[None])


def solution(mesh):
    placed = (
        P("section", ("shard", "replica"), None),
        P("section", ("shard", "replica")),
        P("section", ("shard", "replica"), None),
        P("section", ("shard", "replica")),
        P("section", ("shard", "replica"), None),
        P("section", ("shard", "replica"), None),
        P("section", "shard", None),
        P("section", None),
    )
    return jax.shard_map(
        per_device,
        mesh=mesh,
        in_specs=placed,
        out_specs=(
            P("section", ("shard", "replica"), None),
            P("section", ("shard", "replica"), None),
            P("section", "shard", None),
        ),
        check_vma=False,
    )
```

profile of v0, /device:TPU:0, one launch (start us, length us, event | category | flops | bytes accessed | tf_op | source)
XLA Modules:
  0.0 319.0 jit_solution(15786211053409336877)
XLA Ops:
  7.2 0.0 copy-start.2
  7.2 0.0 copy-start.3
  7.2 0.0 copy-start.4
  7.2 0.0 copy-start.1
  7.2 0.0 copy-start
  7.2 0.0 all-gather.6.cloned.1.call-start
  7.3 0.7 all-gather.6.cloned.1.call-update
  8.0 0.0 reduce-scatter.2.cloned.1.call-start
  8.0 0.1 copy-done.2
  8.1 0.1 reshape.212
  8.2 0.0 copy-done.3
  8.2 0.0 copy-done.4
  8.2 0.3 multiply_cosine_fusion
  8.5 0.1 copy.13
  8.6 0.1 copy.12
  8.7 0.3 multiply_subtract_fusion
  9.0 0.2 maximum_convert_fusion
  9.2 59.8 %all-gather.6.cloned.1.call-done = bf16[1,4096,512]{2,1,0:T(8,128)(2,1)} async-done(((bf16[1,2048,512]{2,1,0:T(8,128)(2,1)}), bf16[1,4096,512]{2,1,0:T(8,128)(2,1)}) %all-gather.6.cloned.1.call-update) | async-done | bytes 4194320 | tf_op jit(solution)/shard_map/all_gather | solution.py:57
  69.1 0.0 copy-done.1
  69.1 0.0 copy-done
  69.1 3.8 %fusion.7 = (f32[128]{0:T(128)S(1)}, f32[128]{0:T(128)S(1)}, f32[128,4096]{1,0:T(8,128)S(1)}) fusion(bf16[1,128,4096]{2,1,0:T(8,128)(2,1)S(1)} %copy-done, f32[4096]{0:T(1024)S(1)} %bitcast.64, bf16[1,4096,512]{2,1,0:T(8,128)(2,1)} %all-gather.6.cloned.1.call-done, bf16[16,8,4,128]{3,2,1,0:T(4,128)(2,1)S(1)} %bitcast.61), kind=kOutput, calls=%fused_computation.14 | convolution fusion | flops 540016384 | bytes 7488512 | tf_op jit(solution)/shard_map/dot_general | solution.py:59
  72.8 1.4 convolution_convert_fusion
  74.2 4.4 %convert_element_type.113 = f32[4096,512]{1,0:T(8,128)} convert(bf16[4096,512]{1,0:T(8,128)(2,1)S(1)} %convolution_convert_fusion) | non-fusion elementwise | flops 2097152 | bytes 12582912 | tf_op jit(solution)/shard_map/convert_element_type | solution.py:82
  78.6 0.0 reduce-scatter.2.cloned.1.call-update
  78.7 0.0 all-gather.4.cloned.1.call-start
  78.7 147.5 %reduce-scatter.2.cloned.1.call-done = f32[512,512]{1,0:T(8,128)} async-done(((f32[4096,512]{1,0:T(8,128)}), f32[512,512]{1,0:T(8,128)}) %reduce-scatter.2.cloned.1.call-update) | async-done | bytes 1048592 | tf_op jit(solution)/shard_map/reduce_scatter | solution.py:81
  226.3 0.0 all-gather.4.cloned.1.call-update
  226.3 2.4 collective-permute-start
  228.7 1.3 collective-permute-start.1
  230.0 0.4 collective-permute-done
  230.4 1.6 fusion.4
  232.0 6.5 %copy.11 = bf16[512,4096]{1,0:T(8,128)(2,1)} copy(bf16[512,4096]{0,1:T(8,128)(2,1)} %bitcast.59) | data formatting | bytes 8388608 | tf_op jit(solution)/shard_map/dot_general | solution.py:58
  238.5 3.8 %fusion.19 = f32[128,4,128]{0,2,1:T(8,128)S(1)} fusion(bf16[4,128,4096]{2,1,0:T(8,128)(2,1)} %bitcast.60, f32[4096]{0:T(1024)S(1)} %bitcast.66, f32[128]{0:T(128)S(1)} %add_rsqrt_fusion.1, bf16[1,128,4096]{2,1,0:T(8,128)(2,1)} %param.8, bf16[1,128,4096]{2,1,0:T(8,128)(2,1)} %collective-permute-done, pred[]{:T(512)S(6)} %eq.6), kind=kOutput, calls=%fused_computation.25 | convolution fusion | flops 539492352 | bytes 6570497 | tf_op jit(solution)/shard_map/dot_general | solution.py:58
  242.4 0.8 copy.14
  243.2 0.0 collective-permute-done.1
  243.2 3.0 fusion.17
  246.2 61.5 %all-gather.4.cloned.1.call-done = f32[2048,512]{1,0:T(8,128)} async-done(((f32[512,512]{1,0:T(8,128)}), f32[2048,512]{1,0:T(8,128)}) %all-gather.4.cloned.1.call-update) | async-done | bytes 4194320 | tf_op jit(solution)/shard_map/all_gather | solution.py:84
  307.7 4.7 %multiply_bitcast_fusion = f32[1,2048,512]{2,1,0:T(8,128)} fusion(f32[2048,512]{1,0:T(8,128)} %all-gather.4.cloned.1.call-done), kind=kLoop, calls=%fused_computation.3 | loop fusion | flops 1048576 | bytes 8388608 | tf_op jit(solution)/shard_map/broadcast_in_dim | solution.py:88
  (7 shorter events, 0.1 us)
Async XLA Ops:
  7.2 0.9 copy-start.2
  7.2 1.0 copy-start.3
  7.2 1.0 copy-start.4
  7.2 61.9 %copy-start.1 = (f32[1,4096]{1,0:T(1,128)S(1)}, f32[1,4096]{1,0:T(1,128)}, u32[]{:S(2)}) copy-start(f32[1,4096]{1,0:T(1,128)} %param.15) | copy-start | bytes 49156
  7.2 61.9 %copy-start = (bf16[1,128,4096]{2,1,0:T(8,128)(2,1)S(1)}, bf16[1,128,4096]{2,1,0:T(8,128)(2,1)}, u32[]{:S(2)}) copy-start(bf16[1,128,4096]{2,1,0:T(8,128)(2,1)} %param.10) | copy-start | bytes 3145732
  7.2 61.8 %all-gather.6.cloned.1.call-start = ((), (), s32[]{:S(2)}) async-start(), calls=%async_computation.3 | async-start | bytes 6291456 | tf_op jit(solution)/shard_map/all_gather | solution.py:57
  8.0 218.3 %reduce-scatter.2.cloned.1.call-start = ((), (), s32[]{:S(2)}) async-start(), calls=%async_computation.1 | async-start | bytes 9437184 | tf_op jit(solution)/shard_map/reduce_scatter | solution.py:81
  78.7 229.1 %all-gather.4.cloned.1.call-start = ((), (), s32[]{:S(2)}) async-start(), calls=%async_computation.2 | async-start | bytes 5242880 | tf_op jit(solution)/shard_map/all_gather | solution.py:84
  226.3 4.1 %collective-permute-start = (bf16[1,128,4096]{2,1,0:T(8,128)(2,1)}, bf16[1,128,4096]{2,1,0:T(8,128)(2,1)}, u32[]{:S(2)}, u32[]{:S(2)}) collective-permute-start(bf16[1,128,4096]{2,1,0:T(8,128)(2,1)} %param.8), channel_id=1, source_target_pairs={{0,8},{8,16},{16,24},{1,9},{9,17},{17,25},{2,10},{10,18},{18,26},{... | collective-permute-start | bytes 3145736 | tf_op jit(solution)/shard_map/ppermute | solution.py:12
  228.7 14.5 %collective-permute-start.1 = (bf16[1,128,4096]{2,1,0:T(8,128)(2,1)}, bf16[1,128,4096]{2,1,0:T(8,128)(2,1)}, u32[]{:S(2)}, u32[]{:S(2)}) collective-permute-start(bf16[1,128,4096]{2,1,0:T(8,128)(2,1)} %param.12), channel_id=1, source_target_pairs={{8,0},{16,8},{24,16},{9,1},{17,9},{25,17},{10,2},{18,10},{26,18},{... | collective-permute-start | bytes 3145736 | tf_op jit(solution)/shard_map/ppermute | solution.py:12
Sparse Core Ops, SparseCore 0:
  9.6 59.4 all-gather.5
  78.8 147.4 reduce-scatter.1
  227.8 79.8 all-gather.3
where the time goes:
time: 319 us
  waiting for transfers between devices  270 us (85%)
  other arithmetic  14.7 us (5%)
  between operations  13.9 us (4%)
  matrix products  8.97 us (3%)
  local copies, waits for them, and re-layouts  7.62 us (2%)
  starting transfers between devices  3.82 us (1%)
    reduce_scatter x1, waiting for transfers between devices, per_device(): lax.psum_scatter(rounded.astype(jnp.float32), ('shard', 'replica'), scatt...  148 us
    all_gather x1, waiting for transfers between devices, per_device(): collected = lax.all_gather(slice_sum, 'replica', axis=0, tiled=True)  61.5 us
    all_gather x1, waiting for transfers between devices, per_device(): gathered = lax.all_gather(local_rows, 'shard', axis=0, tiled=True)  59.8 us
    broadcast_in_dim x2, other arithmetic, per_device(): return (keys[None], grad_out[None], weight_grad[None])  7.73 us
    dot_general x1, local copies, waits for them, and re-layouts, per_device(): projected = jnp.dot(normed, gathered, preferred_element_type=jnp.float32)  6.49 us
  transfers between devices with their start and end apart: 5, of which 4 were waited for; matrix products, arithmetic and copies ran while one was open for 5% of the time, Pallas kernels for 0%

commit v1 on v0

v1 whole, which is shorter than its diff:
```python
import functools

import jax
import jax.numpy as jnp
import numpy as np
from jax import lax
from jax.experimental import pallas as pl
from jax.experimental.pallas import tpu as pltpu
from jax.sharding import PartitionSpec as P

HEAD = 128
THETA = 500000.0
EPS = 1e-05
ROWS = 128
PIECES = 4
SKEW = 2
F32 = jnp.float32
BF16 = jnp.bfloat16
MESH = pl.DeviceIdType.MESH


def kernel(
    X, S, R,
    acts, grads, saved, kcot, w, gain, pos_f, pos_b, rate,
    keys_o, grad_o, wg_o,
    saved_v, kcot_v, w_v, stream_v, arrived_v,
    sv_recv, kg_all, st_recv, g_buf, g_send, p_buf, p_send, p_own,
    part, from_l, from_r, to_r, to_l, go_v, keys_v, inv_v, tab_v,
    lsem, acts_ss, acts_rs, grads_sem, sv_ss, sv_rs, kg_ss, kg_rs,
    st_ss, st_rs, g_ss, g_rs, p_ss, p_rs, r_ss, r_rs, l_ss, l_rs, out_sem,
):
    s, j, r = (lax.axis_index(a) for a in ("section", "shard", "replica"))
    T, D = saved.shape
    N = kcot.shape[1]
    Fs = w.shape[0]
    C = Fs // ROWS
    Fp = Fs // PIECES
    travel = to_r.dtype

    def cols(p, width=Fs, off=0):
        return pl.ds(pl.multiple_of(p * Fs + off, 128), width)

    def peer(d):
        return lax.rem(j + d, S)

    load_saved = pltpu.make_async_copy(saved, saved_v, lsem.at[0])
    load_kcot = pltpu.make_async_copy(kcot, kcot_v, lsem.at[1])
    load_w = pltpu.make_async_copy(w, w_v, lsem.at[2])
    load_acts = pltpu.make_async_copy(acts, stream_v, lsem.at[3])
    load_grads = pltpu.make_async_copy(grads, arrived_v, lsem.at[4])
    load_saved.start()
    load_kcot.start()
    load_w.start()
    pl.when(s == 0)(load_acts.start)
    pl.when(s == X - 1)(load_grads.start)

    barrier = pltpu.get_barrier_semaphore()

    def greet(axis, index):
        pl.semaphore_signal(barrier, inc=1, device_id={axis: index}, device_id_type=MESH)

    for d in range(1, S):
        greet("shard", peer(d))
    pl.when(s > 0)(lambda: greet("section", s - 1))
    pl.when(s < X - 1)(lambda: greet("section", s + 1))
    pl.when(r > 0)(lambda: greet("replica", r - 1))
    pl.when(r < R - 1)(lambda: greet("replica", r + 1))
    peers = S - 1
    for cond in (s > 0, s < X - 1, r > 0, r < R - 1):
        peers = peers + jnp.where(cond, 1, 0)
    pl.semaphore_wait(barrier, peers)

    def remote(src, dst, ss, rs, axis, index):
        return pltpu.make_async_remote_copy(
            src_ref=src, dst_ref=dst, send_sem=ss, recv_sem=rs,
            device_id={axis: index}, device_id_type=MESH,
        )

    def sv_copy(d, q):
        return remote(
            saved.at[:, cols(peer(d), Fp, q * Fp)],
            sv_recv.at[S - d, :, pl.ds(q * Fp, Fp)],
            sv_ss.at[d, q], sv_rs.at[S - d, q], "shard", peer(d),
        )

    def sv_wait(slot, q):
        remote(
            saved.at[:, pl.ds(0, Fp)],
            sv_recv.at[slot, :, pl.ds(pl.multiple_of(q * Fp, 128), Fp)],
            sv_ss.at[slot, q], sv_rs.at[slot, q], "shard", peer(slot),
        ).wait_recv()

    def slot_copy(src, dst, ss, rs, d):
        return remote(src.at[d], dst.at[S - d], ss.at[d], rs.at[S - d], "shard", peer(d))

    def slot_wait(src, dst, ss, rs, slot):
        remote(src.at[slot], dst.at[slot], ss.at[slot], rs.at[slot], "shard", peer(slot)).wait_recv()

    def acts_copy(d):
        return remote(
            acts.at[:, cols(peer(d))], stream_v.at[:, cols(peer(d))],
            acts_ss.at[d], acts_rs.at[d], "section", jnp.minimum(s + 1, X - 1),
        )

    grads_copy = remote(
        grads, arrived_v, grads_sem.at[0], grads_sem.at[1], "section", jnp.maximum(s - 1, 0)
    )

    def kg_copy(d):
        return remote(
            kg_all.at[0], kg_all.at[S - d], kg_ss.at[d], kg_rs.at[S - d], "shard", peer(d)
        )

    def st_copy(d):
        return remote(
            stream_v.at[:, cols(peer(d))], st_recv.at[S - d],
            st_ss.at[d], st_rs.at[S - d], "shard", peer(d),
        )

    def right_copy(c):
        return remote(
            to_r.at[c], from_l.at[c], r_ss.at[c], r_rs.at[c], "replica", jnp.minimum(r + 1, R - 1)
        )

    def left_copy(c):
        return remote(
            to_l.at[c], from_r.at[c], l_ss.at[c], l_rs.at[c], "replica", jnp.maximum(r - 1, 0)
        )

    for d in range(1, S):
        sv_copy(d, 0).start()

    @pl.when(s < X - 1)
    def _():
        for d in (*range(1, S), 0):
            acts_copy(d).start()

    @pl.when(s > 0)
    def _():
        grads_copy.start()

    lane = lax.broadcasted_iota(jnp.int32, (T, HEAD), 1)

    def tables(pos):
        angle = jnp.broadcast_to(pos[...].astype(F32), (T, T)).T[:, :1] * rate[...]
        sine = jnp.sin(angle)
        return jnp.cos(angle), jnp.where(lane < HEAD // 2, -sine, sine)

    def inverse_rms(ref):
        total = jnp.zeros((T, 128), F32)
        for c in range(D // 128):
            v = ref[:, c * 128 : (c + 1) * 128].astype(F32)
            total = total + v * v
        return lax.rsqrt(jnp.sum(total, -1, keepdims=True) / D + EPS)

    cos_b, sin_b = tables(pos_b)
    load_saved.wait()
    load_kcot.wait()
    inverse = inverse_rms(saved_v)
    inv_v[...] = jnp.broadcast_to(inverse, inv_v.shape)
    for h in range(N // HEAD):
        head = slice(h * HEAD, (h + 1) * HEAD)
        v = kcot_v[:, head].astype(F32)
        v = v * cos_b - pltpu.roll(v, HEAD // 2, 1) * sin_b
        kg_all[0, :, head] = (v * inverse).astype(BF16)
    for d in range(1, S):
        kg_copy(d).start()
    for q in range(1, PIECES):
        for d in range(1, S):
            sv_copy(d, q).start()

    cos_f, sin_f = tables(pos_f)
    tab_v[0] = cos_f
    tab_v[1] = sin_f
    for d in range(1, S):
        slot_wait(kg_all, kg_all, kg_ss, kg_rs, d)

    def relay():
        pl.when(s == 0)(load_acts.wait)
        for d in range(1, S):
            pl.when(s > 0)(acts_copy(d).wait_recv)
            st_copy(d).start()

    tile = min(512, Fs)

    def backward():
        load_w.wait()

        @pl.loop(0, Fs // tile)
        def _(i):
            at = pl.ds(pl.multiple_of(i * tile, 128), tile)
            m = lax.dot_general(
                kg_all[...].reshape(S * T, N), w_v[at, :], (((1,), (1,)), ((), ())),
                preferred_element_type=F32,
            )
            m = (m * gain[:, cols(j, tile, i * tile)]).astype(BF16)
            g_buf[0, :, at] = m[:T]
            for d in range(1, S):
                g_send[d, :, at] = m[d * T : (d + 1) * T]

        for d in range(1, S):
            slot_copy(g_send, g_buf, g_ss, g_rs, d).start()

    def project(block):
        total = jnp.zeros((T, N), F32)
        for i in range(Fs // tile):
            g = gain[:, cols(j, tile, i * tile)]
            x = (block(i * tile).astype(F32) * g).astype(BF16)
            total = total + jnp.dot(
                x, w_v[i * tile : (i + 1) * tile, :], preferred_element_type=F32
            )
        return total

    def forward_own():
        pl.when(s > 0)(acts_copy(0).wait_recv)
        p_own[...] = project(lambda o: stream_v[:, cols(j, tile, o)])

    def forward_peers():
        for d in range(1, S):
            remote(
                stream_v.at[:, pl.ds(0, Fs)], st_recv.at[d], st_ss.at[d], st_rs.at[d],
                "shard", peer(d),
            ).wait_recv()
            p_send[d] = project(lambda o: st_recv[d, :, o : o + tile]).astype(p_send.dtype)
            slot_copy(p_send, p_buf, p_ss, p_rs, d).start()

    def finish_grad():
        pl.when(s == X - 1)(load_grads.wait)
        pl.when(s < X - 1)(grads_copy.wait_recv)
        for d in range(1, S):
            slot_wait(g_send, g_buf, g_ss, g_rs, d)
        total = jnp.zeros((T, 128), F32)
        for d in range(S):
            for o in range(0, Fs, 128):
                v = saved_v[:, cols(peer(d), 128, o)].astype(F32)
                total = total + v * g_buf[d, :, o : o + 128].astype(F32)
        inv = inv_v[:, :1]
        factor = inv * inv * (jnp.sum(total, -1, keepdims=True) / D)
        for d in range(S):
            for o in range(0, Fs, 128):
                at = cols(peer(d), 128, o)
                v = saved_v[:, at].astype(F32) * factor
                g = arrived_v[:, at].astype(F32) + g_buf[d, :, o : o + 128].astype(F32)
                go_v[:, at] = (g - v).astype(BF16)
        pltpu.make_async_copy(go_v, grad_o, out_sem.at[C]).start()

    def finish_keys():
        inv = inverse_rms(stream_v)
        for d in range(1, S):
            slot_wait(p_send, p_buf, p_ss, p_rs, d)
        for h in range(N // HEAD):
            head = slice(h * HEAD, (h + 1) * HEAD)
            v = p_own[:, head]
            for d in range(1, S):
                v = v + p_buf[d, :, head].astype(F32)
            v = v * inv
            v = v * tab_v[0] + pltpu.roll(v, HEAD // 2, 1) * tab_v[1]
            keys_v[:, head] = v.astype(BF16)
        pltpu.make_async_copy(keys_v, keys_o, out_sem.at[C + 1]).start()

    scale = float(T * S * R) ** -0.5

    def write_out(c):
        return pltpu.make_async_copy(
            part.at[c], wg_o.at[pl.ds(pl.multiple_of(c * ROWS, ROWS), ROWS), :], out_sem.at[c]
        )

    def when_chunk(c, *conds):
        cond = (c >= 0) & (c < C)
        for extra in conds:
            cond = cond & extra
        return pl.when(cond)

    far = SKEW * jnp.maximum(r, R - 1 - r)
    per_piece = C // PIECES
    tasks = {1: relay, 2: backward, 4: forward_own, 7: forward_peers}
    steps = C + SKEW * (R - 1)

    def step(t, carry):
        @pl.when((t < C) & (lax.rem(t, per_piece) == 0))
        def _():
            for d in range(1, S):
                sv_wait(d, t // per_piece)

        @pl.when(t < C)
        def _():
            g = gain[:, cols(j, ROWS, t * ROWS)]
            blocks = [saved_v[:, cols(j, ROWS, t * ROWS)]]
            for d in range(1, S):
                blocks.append(sv_recv[d, :, pl.ds(pl.multiple_of(t * ROWS, 128), ROWS)])
            x = jnp.concatenate([(b.astype(F32) * g).astype(BF16) for b in blocks], 0)
            part[t] = lax.dot_general(
                x, kg_all[...].reshape(S * T, N), (((0,), (0,)), ((), ())),
                preferred_element_type=F32,
            )

        a = t - SKEW * r

        @when_chunk(a, r == 0, r < R - 1)
        def _():
            to_r[a] = part[a].astype(travel)
            right_copy(a).start()

        @when_chunk(a, r > 0)
        def _():
            right_copy(a).wait_recv()

        @when_chunk(a, r > 0, r < R - 1)
        def _():
            to_r[a] = (part[a] + from_l[a].astype(F32)).astype(travel)
            right_copy(a).start()

        b = t - SKEW * (R - 1 - r)

        @when_chunk(b, r == R - 1, r > 0)
        def _():
            to_l[b] = part[b].astype(travel)
            left_copy(b).start()

        @when_chunk(b, r < R - 1)
        def _():
            left_copy(b).wait_recv()

        @when_chunk(b, r < R - 1, r > 0)
        def _():
            to_l[b] = (part[b] + from_r[b].astype(F32)).astype(travel)
            left_copy(b).start()

        f = t - far

        @when_chunk(f, r > 0)
        def _():
            part[f] = part[f] + from_l[f].astype(F32)

        @when_chunk(f, r < R - 1)
        def _():
            part[f] = part[f] + from_r[f].astype(F32)

        @when_chunk(f)
        def _():
            part[f] = part[f] * scale
            write_out(f).start()

        for at, task in tasks.items():
            pl.when(t == min(at, C - 1))(task)
        pl.when(t == min(13, steps - 1))(finish_grad)
        pl.when(t == min(15, steps - 1))(finish_keys)
        return carry

    lax.fori_loop(0, steps, step, 0)

    for d in range(1, S):
        for q in range(PIECES):
            sv_copy(d, q).wait_send()
        kg_copy(d).wait_send()
        st_copy(d).wait_send()
        slot_copy(g_send, g_buf, g_ss, g_rs, d).wait_send()
        slot_copy(p_send, p_buf, p_ss, p_rs, d).wait_send()

    @pl.when(s < X - 1)
    def _():
        for d in range(S):
            acts_copy(d).wait_send()

    @pl.when(s > 0)
    def _():
        grads_copy.wait_send()

    @pl.loop(0, C)
    def _(c):
        pl.when(r < R - 1)(right_copy(c).wait_send)
        pl.when(r > 0)(left_copy(c).wait_send)
        write_out(c).wait()

    pltpu.make_async_copy(go_v, grad_o, out_sem.at[C]).wait()
    pltpu.make_async_copy(keys_v, keys_o, out_sem.at[C + 1]).wait()


def per_device(acts_fwd, pos_fwd, saved_acts, pos_bwd, grads_in, key_cotan, weight, gain):
    X, S, R = (lax.axis_size(a) for a in ("section", "shard", "replica"))
    T, D = acts_fwd.shape[1:]
    Fs, N = weight.shape[1:]
    C = Fs // ROWS
    travel = BF16 if R <= 8 else F32
    index = np.arange(HEAD) % (HEAD // 2)
    rate = jnp.asarray(THETA ** (-(2.0 * index) / HEAD), F32)[None]
    hbm = pl.BlockSpec(memory_space=pl.ANY)
    vmem = pl.BlockSpec(memory_space=pltpu.VMEM)
    dma = pltpu.SemaphoreType.DMA
    keys, grad_out, weight_grad = pl.pallas_call(
        functools.partial(kernel, X, S, R),
        out_shape=(
            jax.ShapeDtypeStruct((T, N), BF16),
            jax.ShapeDtypeStruct((T, D), BF16),
            jax.ShapeDtypeStruct((Fs, N), F32),
        ),
        in_specs=[hbm] * 5 + [vmem] * 4,
        out_specs=(hbm, hbm, hbm),
        scratch_shapes=[
            pltpu.VMEM((T, D), BF16),
            pltpu.VMEM((T, N), BF16),
            pltpu.VMEM((Fs, N), BF16),
            pltpu.VMEM((T, D), BF16),
            pltpu.VMEM((T, D), BF16),
            pltpu.VMEM((S, T, Fs), BF16),
            pltpu.VMEM((S, T, N), BF16),
            pltpu.VMEM((S, T, Fs), BF16),
            pltpu.VMEM((S, T, Fs), BF16),
            pltpu.VMEM((S, T, Fs), BF16),
            pltpu.VMEM((S, T, N), BF16),
            pltpu.VMEM((S, T, N), BF16),
            pltpu.VMEM((T, N), F32),
            pltpu.VMEM((C, ROWS, N), F32),
            pltpu.VMEM((C, ROWS, N), travel),
            pltpu.VMEM((C, ROWS, N), travel),
            pltpu.VMEM((C, ROWS, N), travel),
            pltpu.VMEM((C, ROWS, N), travel),
            pltpu.VMEM((T, D), BF16),
            pltpu.VMEM((T, N), BF16),
            pltpu.VMEM((T, HEAD), F32),
            pltpu.VMEM((2, T, HEAD), F32),
            dma((5,)),
            dma((S,)), dma((S,)), dma((2,)),
            dma((S, PIECES)), dma((S, PIECES)),
            dma((S,)), dma((S,)),
            dma((S,)), dma((S,)),
            dma((S,)), dma((S,)),
            dma((S,)), dma((S,)),
            dma((C,)), dma((C,)), dma((C,)), dma((C,)),
            dma((C + 2,)),
        ],
        compiler_params=pltpu.CompilerParams(
            collective_id=0, has_side_effects=True, vmem_limit_bytes=60 * 2**20
        ),
        name="relay_window",
    )(
        acts_fwd[0], grads_in[0], saved_acts[0], key_cotan[0], weight[0],
        gain, pos_fwd, pos_bwd, rate,
    )
    return keys[None], grad_out[None], weight_grad[None]


def solution(mesh):
    placed = (
        P("section", ("shard", "replica"), None),
        P("section", ("shard", "replica")),
        P("section", ("shard", "replica"), None),
        P("section", ("shard", "replica")),
        P("section", ("shard", "replica"), None),
        P("section", ("shard", "replica"), None),
        P("section", "shard", None),
        P("section", None),
    )
    return jax.shard_map(
        per_device,
        mesh=mesh,
        in_specs=placed,
        out_specs=(
            P("section", ("shard", "replica"), None),
            P("section", ("shard", "replica"), None),
            P("section", "shard", None),
        ),
        check_vma=False,
    )
```

time: 319 us -> 81.7 us (0.26)
  waiting for transfers between devices: 270 us -> 0 us
  Pallas kernels: 0 us -> 72.3 us
  other arithmetic: 14.7 us -> 0 us
  between operations: 13.9 us -> 0.64 us
  matrix products: 8.97 us -> 0 us
  starting transfers between devices: 3.82 us -> 0 us
    reduce_scatter x1 -> x0, waiting for transfers between devices: 148 us -> none  [per_device(): lax.psum_scatter(rounded.astype(jnp.float32), ('shard', 'replica'), scatt...]
    all_gather x2 -> x0, waiting for transfers between devices: 121 us -> none  [the longest x1 61.5 us: per_device(): collected = lax.all_gather(slice_sum, 'replica', axis=0, tiled=True)]
    pallas_call x0 -> x1, Pallas kernels: none -> 72.3 us  [per_device(): pl.pallas_call(functools.partial(kernel, X, S, R), out_shape=(jax.ShapeDt...]
    dot_general x3 -> x0, matrix products: 8.97 us -> none  [the longest x1 3.83 us: per_device(): projected = jnp.dot(normed, gathered, preferred_element_type=jnp.float32)]
    broadcast_in_dim x2 -> x0, other arithmetic: 7.73 us -> none  [per_device(): return (keys[None], grad_out[None], weight_grad[None])]
    unnamed x11 -> x3, local copies, waits for them, and re-layouts: 0.86 us -> 8.49 us
    dot_general x1 -> x0, local copies, waits for them, and re-layouts: 6.49 us -> none  [per_device(): projected = jnp.dot(normed, gathered, preferred_element_type=jnp.float32)]
    convert_element_type x3 -> x0, other arithmetic: 4.61 us -> none  [the longest x1 4.43 us: per_device(): rounded.astype(jnp.float32)]
  transfers between devices with their start and end apart: 5 -> 0, of which waited for: 4 -> 0; matrix products, arithmetic and copies ran while one was open for 5% -> 0% of each run, Pallas kernels for 0% -> 0%
where the time goes in v1:
time: 81.7 us; the launch traced here: 81.4 us
  Pallas kernels  72.3 us (88%)
  local copies, waits for them, and re-layouts  8.49 us (10%)
    pallas_call x1, Pallas kernels, per_device(): pl.pallas_call(functools.partial(kernel, X, S, R), out_shape=(jax.ShapeDt...  72.3 us
    unnamed x3, local copies, waits for them, and re-layouts  8.49 us

profile of v1, /device:TPU:0, one launch (start us, length us, event | category | flops | bytes accessed | tf_op | source)
XLA Modules:
  0.0 81.4 jit_solution(17532803527097930044)
XLA Ops:
  0.6 72.3 %relay_window.1 = (bf16[128,512]{1,0:T(8,128)(2,1)}, bf16[128,4096]{1,0:T(8,128)(2,1)}, f32[2048,512]{1,0:T(8,128)}) custom-call(bf16[128,4096]{1,0:T(8,128)(2,1)} %bitcast.11, bf16[128,4096]{1,0:T(8,128)(2,1)} %bitcast.12, bf16[128,4096]{1,0:T(8,128)(2,1)} %bitcast.13, bf16[128,512]{1,0:T(8,128)(2,1)} %bitcast.14, bf16[2048,512]{1,0:T(8,128)(2,1)} %bitcast.9, ...), custom_call_target="tpu_custom_call" | custom-call | tf_op jit(solution)/shard_map/relay_window/pallas_call | solution.py:390
  72.9 1.6 %copy.15 = bf16[1,128,512]{2,1,0:T(8,128)(2,1)} copy(bf16[1,128,512]{2,1,0:T(8,128)(2,1)} %bitcast.15) | data formatting | bytes 262144
  74.5 2.3 %copy.16 = bf16[1,128,4096]{2,1,0:T(8,128)(2,1)} copy(bf16[1,128,4096]{2,1,0:T(8,128)(2,1)} %bitcast.10) | data formatting | bytes 2097152
  76.8 4.6 %copy.17 = f32[1,2048,512]{2,1,0:T(8,128)} copy(f32[1,2048,512]{2,1,0:T(8,128)} %bitcast.8) | data formatting | bytes 8388608

commit v2 on v1

--- a/solution.py
+++ b/solution.py
@@ -12,8 +12,9 @@
 THETA = 500000.0
 EPS = 1e-05
 ROWS = 128
-PIECES = 4
-SKEW = 2
+PARTS = 2
+PIECES = 8
+SKEW = 3
 F32 = jnp.float32
 BF16 = jnp.bfloat16
 MESH = pl.DeviceIdType.MESH
@@ -25,16 +26,19 @@
     keys_o, grad_o, wg_o,
     saved_v, kcot_v, w_v, stream_v, arrived_v,
     sv_recv, kg_all, st_recv, g_buf, g_send, p_buf, p_send, p_own,
-    part, from_l, from_r, to_r, to_l, go_v, keys_v, inv_v, tab_v,
+    part, from_l, from_r, to_r, to_l, inv_v, tab_v,
     lsem, acts_ss, acts_rs, grads_sem, sv_ss, sv_rs, kg_ss, kg_rs,
-    st_ss, st_rs, g_ss, g_rs, p_ss, p_rs, r_ss, r_rs, l_ss, l_rs, out_sem,
+    st_ss, st_rs, g_ss, g_rs, p_ss, p_rs, r_ss, r_rs, l_ss, l_rs,
 ):
     s, j, r = (lax.axis_index(a) for a in ("section", "shard", "replica"))
     T, D = saved.shape
     N = kcot.shape[1]
     Fs = w.shape[0]
-    C = Fs // ROWS
-    Fp = Fs // PIECES
+    blocks = Fs // ROWS
+    C = blocks * PARTS
+    width = N // PARTS
+    pieces = min(PIECES, blocks)
+    Fp = Fs // pieces
     travel = to_r.dtype
 
     def cols(p, width=Fs, off=0):
@@ -165,7 +169,7 @@
         kg_all[0, :, head] = (v * inverse).astype(BF16)
     for d in range(1, S):
         kg_copy(d).start()
-    for q in range(1, PIECES):
+    for q in range(1, pieces):
         for d in range(1, S):
             sv_copy(d, q).start()
 
@@ -241,8 +245,7 @@
                 at = cols(peer(d), 128, o)
                 v = saved_v[:, at].astype(F32) * factor
                 g = arrived_v[:, at].astype(F32) + g_buf[d, :, o : o + 128].astype(F32)
-                go_v[:, at] = (g - v).astype(BF16)
-        pltpu.make_async_copy(go_v, grad_o, out_sem.at[C]).start()
+                grad_o[:, at] = (g - v).astype(BF16)
 
     def finish_keys():
         inv = inverse_rms(stream_v)
@@ -255,15 +258,9 @@
                 v = v + p_buf[d, :, head].astype(F32)
             v = v * inv
             v = v * tab_v[0] + pltpu.roll(v, HEAD // 2, 1) * tab_v[1]
-            keys_v[:, head] = v.astype(BF16)
-        pltpu.make_async_copy(keys_v, keys_o, out_sem.at[C + 1]).start()
+            keys_o[:, head] = v.astype(BF16)
 
     scale = float(T * S * R) ** -0.5
-
-    def write_out(c):
-        return pltpu.make_async_copy(
-            part.at[c], wg_o.at[pl.ds(pl.multiple_of(c * ROWS, ROWS), ROWS), :], out_sem.at[c]
-        )
 
     def when_chunk(c, *conds):
         cond = (c >= 0) & (c < C)
@@ -272,8 +269,8 @@
         return pl.when(cond)
 
     far = SKEW * jnp.maximum(r, R - 1 - r)
-    per_piece = C // PIECES
-    tasks = {1: relay, 2: backward, 4: forward_own, 7: forward_peers}
+    per_piece = C // pieces
+    tasks = {2: relay, 4: backward, 8: forward_own, 14: forward_peers}
     steps = C + SKEW * (R - 1)
 
     def step(t, carry):
@@ -282,17 +279,20 @@
             for d in range(1, S):
                 sv_wait(d, t // per_piece)
 
-        @pl.when(t < C)
-        def _():
-            g = gain[:, cols(j, ROWS, t * ROWS)]
-            blocks = [saved_v[:, cols(j, ROWS, t * ROWS)]]
+        @pl.when((t < C) & (lax.rem(t, PARTS) == 0))
+        def _():
+            o = (t // PARTS) * ROWS
+            g = gain[:, cols(j, ROWS, o)]
+            sides = [saved_v[:, cols(j, ROWS, o)]]
             for d in range(1, S):
-                blocks.append(sv_recv[d, :, pl.ds(pl.multiple_of(t * ROWS, 128), ROWS)])
-            x = jnp.concatenate([(b.astype(F32) * g).astype(BF16) for b in blocks], 0)
-            part[t] = lax.dot_general(
+                sides.append(sv_recv[d, :, pl.ds(pl.multiple_of(o, 128), ROWS)])
+            x = jnp.concatenate([(v.astype(F32) * g).astype(BF16) for v in sides], 0)
+            term = lax.dot_general(
                 x, kg_all[...].reshape(S * T, N), (((0,), (0,)), ((), ())),
                 preferred_element_type=F32,
             )
+            for h in range(PARTS):
+                part[t + h] = term[:, h * width : (h + 1) * width]
 
         a = t - SKEW * r
 
@@ -328,29 +328,30 @@
 
         f = t - far
 
-        @when_chunk(f, r > 0)
-        def _():
-            part[f] = part[f] + from_l[f].astype(F32)
-
-        @when_chunk(f, r < R - 1)
-        def _():
-            part[f] = part[f] + from_r[f].astype(F32)
-
-        @when_chunk(f)
-        def _():
-            part[f] = part[f] * scale
-            write_out(f).start()
+        def finish(*sums):
+            rows = pl.ds(pl.multiple_of((f // PARTS) * ROWS, ROWS), ROWS)
+            at = pl.ds(pl.multiple_of(lax.rem(f, PARTS) * width, 128), width)
+            total = part[f]
+            for ref in sums:
+                total = total + ref[f].astype(F32)
+            wg_o[rows, at] = total * scale
+
+        when_chunk(f, r == 0, r < R - 1)(lambda: finish(from_r))
+        when_chunk(f, r > 0, r < R - 1)(lambda: finish(from_l, from_r))
+        when_chunk(f, r > 0, r == R - 1)(lambda: finish(from_l))
+        if R == 1:
+            when_chunk(f)(finish)
 
         for at, task in tasks.items():
             pl.when(t == min(at, C - 1))(task)
-        pl.when(t == min(13, steps - 1))(finish_grad)
-        pl.when(t == min(15, steps - 1))(finish_keys)
+        pl.when(t == min(26, steps - 1))(finish_grad)
+        pl.when(t == min(30, steps - 1))(finish_keys)
         return carry
 
     lax.fori_loop(0, steps, step, 0)
 
     for d in range(1, S):
-        for q in range(PIECES):
+        for q in range(pieces):
             sv_copy(d, q).wait_send()
         kg_copy(d).wait_send()
         st_copy(d).wait_send()
@@ -370,32 +371,41 @@
     def _(c):
         pl.when(r < R - 1)(right_copy(c).wait_send)
         pl.when(r > 0)(left_copy(c).wait_send)
-        write_out(c).wait()
-
-    pltpu.make_async_copy(go_v, grad_o, out_sem.at[C]).wait()
-    pltpu.make_async_copy(keys_v, keys_o, out_sem.at[C + 1]).wait()
+
+
+def store_kernel(a, b, c, a_out, b_out, c_out, sem):
+    copies = [
+        pltpu.make_async_copy(src, dst, sem.at[i])
+        for i, (src, dst) in enumerate(((c, c_out), (b, b_out), (a, a_out)))
+    ]
+    for copy in copies:
+        copy.start()
+    for copy in copies:
+        copy.wait()
 
 
 def per_device(acts_fwd, pos_fwd, saved_acts, pos_bwd, grads_in, key_cotan, weight, gain):
     X, S, R = (lax.axis_size(a) for a in ("section", "shard", "replica"))
     T, D = acts_fwd.shape[1:]
     Fs, N = weight.shape[1:]
-    C = Fs // ROWS
+    C = Fs // ROWS * PARTS
+    width = N // PARTS
+    pieces = min(PIECES, Fs // ROWS)
     travel = BF16 if R <= 8 else F32
     index = np.arange(HEAD) % (HEAD // 2)
     rate = jnp.asarray(THETA ** (-(2.0 * index) / HEAD), F32)[None]
-    hbm = pl.BlockSpec(memory_space=pl.ANY)
+    hbm = pl.BlockSpec(memory_space=pltpu.HBM)
     vmem = pl.BlockSpec(memory_space=pltpu.VMEM)
     dma = pltpu.SemaphoreType.DMA
-    keys, grad_out, weight_grad = pl.pallas_call(
+    results = pl.pallas_call(
         functools.partial(kernel, X, S, R),
         out_shape=(
-            jax.ShapeDtypeStruct((T, N), BF16),
-            jax.ShapeDtypeStruct((T, D), BF16),
-            jax.ShapeDtypeStruct((Fs, N), F32),
+            pltpu.VMEM((T, N), BF16),
+            pltpu.VMEM((T, D), BF16),
+            pltpu.VMEM((Fs, N), F32),
         ),
         in_specs=[hbm] * 5 + [vmem] * 4,
-        out_specs=(hbm, hbm, hbm),
+        out_specs=(vmem, vmem, vmem),
         scratch_shapes=[
             pltpu.VMEM((T, D), BF16),
             pltpu.VMEM((T, N), BF16),
@@ -410,33 +420,39 @@
             pltpu.VMEM((S, T, N), BF16),
             pltpu.VMEM((S, T, N), BF16),
             pltpu.VMEM((T, N), F32),
-            pltpu.VMEM((C, ROWS, N), F32),
-            pltpu.VMEM((C, ROWS, N), travel),
-            pltpu.VMEM((C, ROWS, N), travel),
-            pltpu.VMEM((C, ROWS, N), travel),
-            pltpu.VMEM((C, ROWS, N), travel),
-            pltpu.VMEM((T, D), BF16),
-            pltpu.VMEM((T, N), BF16),
+            pltpu.VMEM((C, ROWS, width), F32),
+            pltpu.VMEM((C, ROWS, width), travel),
+            pltpu.VMEM((C, ROWS, width), travel),
+            pltpu.VMEM((C, ROWS, width), travel),
+            pltpu.VMEM((C, ROWS, width), travel),
             pltpu.VMEM((T, HEAD), F32),
             pltpu.VMEM((2, T, HEAD), F32),
             dma((5,)),
             dma((S,)), dma((S,)), dma((2,)),
-            dma((S, PIECES)), dma((S, PIECES)),
+            dma((S, pieces)), dma((S, pieces)),
             dma((S,)), dma((S,)),
             dma((S,)), dma((S,)),
             dma((S,)), dma((S,)),
             dma((S,)), dma((S,)),
             dma((C,)), dma((C,)), dma((C,)), dma((C,)),
-            dma((C + 2,)),
         ],
         compiler_params=pltpu.CompilerParams(
-            collective_id=0, has_side_effects=True, vmem_limit_bytes=60 * 2**20
+            collective_id=0, has_side_effects=True, vmem_limit_bytes=int(57.8 * 2**20)
         ),
         name="relay_window",
     )(
         acts_fwd[0], grads_in[0], saved_acts[0], key_cotan[0], weight[0],
         gain, pos_fwd, pos_bwd, rate,
     )
+    keys, grad_out, weight_grad = pl.pallas_call(
+        store_kernel,
+        out_shape=tuple(jax.ShapeDtypeStruct(v.shape, v.dtype) for v in results),
+        in_specs=[vmem] * 3,
+        out_specs=[hbm] * 3,
+        scratch_shapes=[dma((3,))],
+        compiler_params=pltpu.CompilerParams(vmem_limit_bytes=8 * 2**20),
+        name="store_results",
+    )(*results)
     return keys[None], grad_out[None], weight_grad[None]
 
 

time: 81.7 us -> 72.4 us (0.89)
  local copies, waits for them, and re-layouts: 8.49 us -> 0 us
    unnamed x3 -> x0, local copies, waits for them, and re-layouts: 8.49 us -> none
    pallas_call x1 -> x2, Pallas kernels: 72.3 us -> 71.6 us  [the longest x1 69.3 us: per_device(): pl.pallas_call(functools.partial(kernel, X, S, R), out_shape=(pltpu.VMEM(...]
where the time goes in v2:
time: 72.4 us; the launch traced here: 72.3 us
  Pallas kernels  71.6 us (99%)
    pallas_call x1, Pallas kernels, per_device(): pl.pallas_call(functools.partial(kernel, X, S, R), out_shape=(pltpu.VMEM(...  69.3 us
    pallas_call x1, Pallas kernels, per_device(): pl.pallas_call(store_kernel, out_shape=tuple((jax.ShapeDtypeStruct(v.shap...  2.38 us

profile of v2, /device:TPU:0, one launch (start us, length us, event | category | flops | bytes accessed | tf_op | source)
XLA Modules:
  0.0 72.3 jit_solution(16884447667577061664)
XLA Ops:
  0.6 69.3 %relay_window.1 = (bf16[128,512]{1,0:T(8,128)(2,1)S(1)}, bf16[128,4096]{1,0:T(8,128)(2,1)S(1)}, f32[2048,512]{1,0:T(8,128)S(1)}) custom-call(bf16[128,4096]{1,0:T(8,128)(2,1)} %bitcast.9, bf16[128,4096]{1,0:T(8,128)(2,1)} %bitcast.10, bf16[128,4096]{1,0:T(8,128)(2,1)} %bitcast.11, bf16[128,512]{1,0:T(8,128)(2,1)} %bitcast.12, bf16[2048,512]{1,0:T(8,128)(2,1)} %bitcast.8, ...), custom_call_target="tpu_custom_call" | custom-call | tf_op jit(solution)/shard_map/relay_window/pallas_call | solution.py:400
  69.9 2.4 %store_results.1 = (bf16[128,512]{1,0:T(8,128)(2,1)}, bf16[128,4096]{1,0:T(8,128)(2,1)}, f32[2048,512]{1,0:T(8,128)}) custom-call(bf16[128,512]{1,0:T(8,128)(2,1)S(1)} %get-tuple-element.9.a, bf16[128,4096]{1,0:T(8,128)(2,1)S(1)} %get-tuple-element.10.b, f32[2048,512]{1,0:T(8,128)S(1)} %get-tuple-element.11.c), custom_call_target="tpu_custom_call" | custom-call | tf_op jit(solution)/shard_map/store_results/pallas_call | solution.py:447
